TPU v7x, 256 devices: a whole 4x4x8 slice. The times are simulated.
256 devices in a mesh: batch: 32 (over z_hi, y, core), gene: 8 (over x, z_lo).
Axes of the slice: x: 4, y: 4, z: 8 (z_hi: 4, z_lo: 2; z = z_hi * 2 + z_lo), core: 2. Of those that a mesh axis runs over, the one named last changes fastest.
Arguments:
- umi_counts: int32 [32768, 8192], P('batch', 'gene'), may hold values from 0 to 65535
- cell_donors: int32 [32768], P('batch'), may hold values from 0 to 127
- cell_types: int32 [32768], P('batch'), may hold values from 0 to 23
- live_cells: int32 [32], P('batch'), may hold values from 1 to 1024, 20480 in all
- dosages: int32 [128, 4096], P(None, 'batch'), may hold values from 0 to 2
Outputs:
- scores: bfloat16 [24, 8192, 4096], P(None, ('gene', 'batch'))
All inputs are finite; a program needn't handle non-finite values. No bound on the sum of `live_cells` on one device may be relied on, other than what follows from the above.
Results may differ from a plain program's by a relative error of at most 0.0069.
Values may be sent and summed in bfloat16 or wider, within the bound.
A program may use at most 128 MiB of HBM per device.

v0:
```python
import jax
import jax.numpy as jnp
from jax import lax
from jax.sharding import Mesh
from jax.sharding import PartitionSpec as P

TYPES = 24
DONORS = 128
BATCH = ("batch_0", "batch_1", "batch_2")
BATCH_GENE = ("batch_0", "batch_1", "batch_2", "gene_0", "gene_1")
GENE = ("gene_0", "gene_1")
GENE_BATCH = ("gene_0", "gene_1", "batch_0", "batch_1", "batch_2")


def in_blocks(value, dim, count):
    dims = value.shape
    tiles = value.reshape(*dims[:dim], count, dims[dim] // count, *dims[dim + 1 :])
    return jnp.moveaxis(tiles, dim, 0)


def summed_rows_2(value, chips, core, dim):
    sizes = (lax.axis_size(chips), lax.axis_size(core))
    tiles = in_blocks(value, dim, sizes[0] * sizes[1])
    inside = tiles.shape[1:]
    tiles = tiles.reshape(*sizes, *inside).swapaxes(0, 1).reshape(-1, *inside)
    tiles = lax.psum_scatter(tiles, core, scatter_dimension=0, tiled=True)
    return lax.psum_scatter(tiles, chips, scatter_dimension=0, tiled=True)[0]


def one_axis_at_a_time(value, axes):
    for axis in axes:
        value = lax.psum(value, axis)
    return value


def one_hot_rows(group_ids, total_groups):
    columns = jnp.arange(total_groups, dtype=jnp.int32)
    return (group_ids[:, None] == columns[None, :]).astype(jnp.bfloat16)


def standardize_dosage(block_dosage):
    genotype = block_dosage.astype(jnp.float32)
    centred = genotype - jnp.mean(genotype, axis=0, keepdims=True)
    return (centred * lax.rsqrt(jnp.mean(centred * centred, axis=0, keepdims=True) + 1e-06)).astype(
        jnp.bfloat16
    )


def on_device(umi_counts, cell_donors, cell_types, live_cells, dosages):
    total_groups = TYPES * DONORS
    cell_slots = umi_counts.shape[0]
    genes_block = umi_counts.shape[1]
    batch_count = lax.axis_size(BATCH)
    genes_local = genes_block // batch_count
    slot_index = jnp.arange(cell_slots, dtype=jnp.int32)
    alive_mask = slot_index < live_cells[0]
    cell_group = jnp.where(alive_mask, cell_types * DONORS + cell_donors, -1)
    rounded = umi_counts.astype(jnp.bfloat16)
    table = one_hot_rows(cell_group, total_groups)
    pseudo = summed_rows_2(
        lax.dot_general(
            rounded, table, (((0,), (0,)), ((), ())), preferred_element_type=jnp.float32
        ),
        ("batch_0", "batch_1"),
        "batch_2",
        0,
    )
    partial_library = jnp.sum(pseudo, axis=0)
    library = jnp.maximum(one_axis_at_a_time(partial_library, BATCH_GENE), 1.0)
    logged = jnp.log1p(10000.0 * pseudo / library[None, :]).reshape(genes_local, TYPES, DONORS)
    centred = logged - jnp.mean(logged, axis=2, keepdims=True)
    standard = (
        centred * lax.rsqrt(jnp.mean(centred * centred, axis=2, keepdims=True) + 1e-06)
    ).astype(jnp.bfloat16)
    standard_rows = jnp.transpose(standard, (1, 0, 2)).reshape(TYPES * genes_local, DONORS)
    factor = DONORS ** (-0.5)
    geno_local = standardize_dosage(dosages)
    geno_piece = lax.all_gather(geno_local, BATCH, axis=1, tiled=True)
    product = jnp.dot(standard_rows, geno_piece, preferred_element_type=jnp.float32) * factor
    return product.reshape(TYPES, genes_local, geno_piece.shape[1]).astype(jnp.bfloat16)


def solution(mesh):
    torus = Mesh(
        mesh.devices.reshape(4, 4, 2, 4, 2), ("batch_0", "batch_1", "batch_2", "gene_0", "gene_1")
    )
    return jax.shard_map(
        on_device,
        mesh=torus,
        in_specs=(P(BATCH, GENE), P(BATCH), P(BATCH), P(BATCH), P(None, BATCH)),
        out_specs=P(None, GENE_BATCH, None),
        check_vma=False,
    )
```

profile of v0, /device:TPU:32, one launch (start us, length us, event | category | flops | bytes accessed | tf_op | source)
XLA Modules:
  0.0 256.0 jit_solution(15902992954588551847)
XLA Ops:
  8.0 0.7 add_select_fusion
  8.7 12.0 %fusion = f32[3072,1024]{0,1:T(8,128)} fusion(s32[1024]{0:T(1024)S(1)} %add_select_fusion, s32[1024,1024]{1,0:T(8,128)} %param.5), kind=kOutput, calls=%fused_computation.2 | convolution fusion | flops 6446645248 | bytes 16781312 | tf_op jit(solution)/shard_map/dot_general | solution.py:61
  20.7 10.8 %copy.6 = f32[16,2,32,3072]{3,2,0,1:T(8,128)} copy(f32[16,2,32,3072]{3,2,1,0:T(8,128)} %bitcast.21) | data formatting | bytes 25165824 | tf_op jit(solution)/shard_map/reshape;reshape | solution.py:25
  31.5 0.0 reduce-scatter.3.cloned.1.call-update
  31.5 0.0 copy-start
  31.6 0.0 reduce-scatter.5.cloned.1.call-start
  31.6 30.0 %reduce-scatter.3.cloned.1.call-done = f32[16,32,3072]{2,1,0:T(8,128)} async-done(((f32[32,32,3072]{2,1,0:T(8,128)}), f32[16,32,3072]{2,1,0:T(8,128)}) %reduce-scatter.3.cloned.1.call-update) | async-done | bytes 6291472 | tf_op jit(solution)/shard_map/reduce_scatter | solution.py:26
  61.6 0.0 reduce-scatter.5.cloned.1.call-update
  61.6 0.0 all-gather.2.cloned.1.call-start
  61.8 0.6 multiply_convert_fusion.2
  62.4 0.0 all-gather.2.cloned.1.call-update
  62.4 114.4 %reduce-scatter.5.cloned.1.call-done = f32[1,32,3072]{2,1,0:T(8,128)} async-done(((f32[16,32,3072]{2,1,0:T(8,128)}), f32[1,32,3072]{2,1,0:T(8,128)}) %reduce-scatter.5.cloned.1.call-update) | async-done | bytes 393232 | tf_op jit(solution)/shard_map/reduce_scatter | solution.py:27
  176.9 1.0 multiply_bitcast_fusion
  177.9 0.1 copy.8
  178.0 19.5 %psum.35 = f32[3072]{0:T(1024)S(1)} all-reduce(f32[3072]{0:T(1024)S(1)} %get-tuple-element.6), channel_id=1, replica_groups=mesh['batch_0'=4,'batch_1'=4,'batch_2'=2,'gene_0'=4,'gene_1'=2] {'batch_0'}, use_global_device_ids=true, to_apply=%region_3.4 | all-reduce | flops 3072 | bytes 24576 | tf_op jit(solution)/shard_map/psum | solution.py:32
  197.5 15.9 %psum.36 = f32[3072]{0:T(1024)S(1)} all-reduce(f32[3072]{0:T(1024)S(1)} %psum.35), channel_id=1, replica_groups=mesh['batch_0'=4,'batch_1'=4,'batch_2'=2,'gene_0'=4,'gene_1'=2] {'batch_1'}, use_global_device_ids=true, to_apply=%region_4.5 | all-reduce | flops 3072 | bytes 24576 | tf_op jit(solution)/shard_map/psum | solution.py:32
  213.3 3.3 %psum.37 = f32[3072]{0:T(1024)S(1)} all-reduce(f32[3072]{0:T(1024)S(1)} %psum.36), channel_id=1, replica_groups=mesh['batch_0'=4,'batch_1'=4,'batch_2'=2,'gene_0'=4,'gene_1'=2] {'batch_2'}, use_global_device_ids=true, to_apply=%region_5.6 | all-reduce | flops 3072 | bytes 24576 | tf_op jit(solution)/shard_map/psum | solution.py:32
  216.6 16.8 %psum.38 = f32[3072]{0:T(1024)S(1)} all-reduce(f32[3072]{0:T(1024)S(1)} %psum.37), channel_id=1, replica_groups=mesh['batch_0'=4,'batch_1'=4,'batch_2'=2,'gene_0'=4,'gene_1'=2] {'gene_0'}, use_global_device_ids=true, to_apply=%region_6.7 | all-reduce | flops 3072 | bytes 24576 | tf_op jit(solution)/shard_map/psum | solution.py:32
  233.4 8.5 %psum.39 = f32[3072]{0:T(1024)S(1)} all-reduce(f32[3072]{0:T(1024)S(1)} %psum.38), channel_id=1, replica_groups=mesh['batch_0'=4,'batch_1'=4,'batch_2'=2,'gene_0'=4,'gene_1'=2] {'gene_1'}, use_global_device_ids=true, to_apply=%region_7.8 | all-reduce | flops 3072 | bytes 24576 | tf_op jit(solution)/shard_map/psum | solution.py:32
  241.9 0.2 fusion.4
  242.1 0.3 multiply_reduce_fusion
  242.5 0.3 multiply_convert_fusion.1
  242.8 0.0 all-gather.2.cloned.1.call-done
  242.8 5.7 %multiply_convert_fusion = bf16[768,4096]{1,0:T(8,128)(2,1)} fusion(bf16[768,128]{1,0:T(8,128)(2,1)S(1)} %bitcast.25, bf16[128,4096]{1,0:T(8,128)(2,1)} %all-gather.2.cloned.1.call-done), kind=kOutput, calls=%fused_computation | convolution fusion | flops 811597824 | bytes 7536640 | tf_op jit(solution)/shard_map/dot_general | solution.py:79
  (9 shorter events, 0.1 us)
Async XLA Ops:
  7.4 54.2 %reduce-scatter.3.cloned.1.call-start = ((), (), s32[]{:S(2)}) async-start(), calls=%async_computation.2 | async-start | bytes 18874368 | tf_op jit(solution)/shard_map/reduce_scatter | solution.py:26
  31.5 30.1 %copy-start = (s32[128,128]{1,0:T(8,128)S(1)}, s32[128,128]{1,0:T(8,128)}, u32[]{:S(2)}) copy-start(s32[128,128]{1,0:T(8,128)} %param.9) | copy-start | bytes 196612
  31.6 145.3 %reduce-scatter.5.cloned.1.call-start = ((), (), s32[]{:S(2)}) async-start(), calls=%async_computation.3 | async-start | bytes 6684672 | tf_op jit(solution)/shard_map/reduce_scatter | solution.py:27
  61.6 181.2 %all-gather.2.cloned.1.call-start = ((), (), s32[]{:S(2)}) async-start(), calls=%async_computation.4 | async-start | bytes 1081344 | tf_op jit(solution)/shard_map/all_gather | solution.py:78
Sparse Core Ops, SparseCore 0:
  31.7 29.8 reduce-scatter.2
  65.3 111.5 reduce-scatter.4
Sparse Core Ops, SparseCore 1:
  64.6 63.7 all-gather.1
where the time goes:
time: 256 us
  waiting for transfers between devices  145 us (57%)
  blocking collectives  63.9 us (25%)
  matrix products  17.7 us (7%)
  between operations  15.6 us (6%)
  local copies, waits for them, and re-layouts  10.9 us (4%)
  other arithmetic  3.33 us (1%)
    reduce_scatter x1, waiting for transfers between devices, summed_rows_2(): return lax.psum_scatter(tiles, chips, scatter_dimension=0, tiled=True)[0]  114 us
    psum x5, blocking collectives, one_axis_at_a_time(): value = lax.psum(value, axis)  63.9 us
    reduce_scatter x1, waiting for transfers between devices, summed_rows_2(): tiles = lax.psum_scatter(tiles, core, scatter_dimension=0, tiled=True)  30 us
    dot_general x1, matrix products, on_device(): lax.dot_general(rounded, table, (((0,), (0,)), ((), ())), preferred_eleme...  12 us
    another operation x1, local copies, waits for them, and re-layouts, summed_rows_2(): tiles = tiles.reshape(*sizes, *inside).swapaxes(0, 1).reshape(-1, *inside)  10.8 us
    dot_general x1, matrix products, on_device(): jnp.dot(standard_rows, geno_piece, preferred_element_type=jnp.float32)  5.72 us
  transfers between devices with their start and end apart: 3, of which 2 were waited for; matrix products, arithmetic and copies ran while one was open for 1% of the time, Pallas kernels for 0%

commit v1 on v0

--- a/solution.py
+++ b/solution.py
@@ -29,7 +29,7 @@
 
 def one_axis_at_a_time(value, axes):
     for axis in axes:
-        value = lax.psum(value, axis)
+        value = jnp.sum(lax.all_gather(value, axis_name=axis), axis=0)
     return value
 
 

time: 256 us -> 238 us (0.930)
  blocking collectives: 63.9 us -> 45 us
    psum x5 -> x0, blocking collectives: 63.9 us -> none  [one_axis_at_a_time(): value = lax.psum(value, axis)]
    all_gather x0 -> x5, blocking collectives: none -> 45 us  [one_axis_at_a_time(): value = jnp.sum(lax.all_gather(value, axis_name=axis), axis=0)]
where the time goes in v1:
time: 238 us; the launch traced here: 237 us
  waiting for transfers between devices  145 us (61%)
  blocking collectives  45 us (19%)
  matrix products  17.7 us (7%)
  between operations  15.6 us (7%)
  local copies, waits for them, and re-layouts  11 us (5%)
  other arithmetic  3.49 us (1%)
    reduce_scatter x1, waiting for transfers between devices, summed_rows_2(): return lax.psum_scatter(tiles, chips, scatter_dimension=0, tiled=True)[0]  114 us
    all_gather x5, blocking collectives, one_axis_at_a_time(): value = jnp.sum(lax.all_gather(value, axis_name=axis), axis=0)  45 us
    reduce_scatter x1, waiting for transfers between devices, summed_rows_2(): tiles = lax.psum_scatter(tiles, core, scatter_dimension=0, tiled=True)  30 us
    dot_general x1, matrix products, on_device(): lax.dot_general(rounded, table, (((0,), (0,)), ((), ())), preferred_eleme...  12 us
    another operation x1, local copies, waits for them, and re-layouts, summed_rows_2(): tiles = tiles.reshape(*sizes, *inside).swapaxes(0, 1).reshape(-1, *inside)  10.8 us
    dot_general x1, matrix products, on_device(): jnp.dot(standard_rows, geno_piece, preferred_element_type=jnp.float32)  5.72 us
  transfers between devices with their start and end apart: 3, of which 2 were waited for; matrix products, arithmetic and copies ran while one was open for 1% of the time, Pallas kernels for 0%

profile of v1, /device:TPU:32, one launch (start us, length us, event | category | flops | bytes accessed | tf_op | source)
XLA Modules:
  0.0 237.4 jit_solution(6640719165067442575)
XLA Ops:
  8.0 0.7 add_select_fusion
  8.7 12.0 %fusion = f32[3072,1024]{0,1:T(8,128)} fusion(s32[1024]{0:T(1024)S(1)} %add_select_fusion, s32[1024,1024]{1,0:T(8,128)} %param.5), kind=kOutput, calls=%fused_computation.2 | convolution fusion | flops 6446645248 | bytes 16781312 | tf_op jit(solution)/shard_map/dot_general | solution.py:61
  20.7 10.8 %copy.10 = f32[16,2,32,3072]{3,2,0,1:T(8,128)} copy(f32[16,2,32,3072]{3,2,1,0:T(8,128)} %bitcast.21) | data formatting | bytes 25165824 | tf_op jit(solution)/shard_map/reshape;reshape | solution.py:25
  31.5 0.0 reduce-scatter.3.cloned.1.call-update
  31.5 0.0 copy-start
  31.6 0.0 reduce-scatter.5.cloned.1.call-start
  31.6 30.0 %reduce-scatter.3.cloned.1.call-done = f32[16,32,3072]{2,1,0:T(8,128)} async-done(((f32[32,32,3072]{2,1,0:T(8,128)}), f32[16,32,3072]{2,1,0:T(8,128)}) %reduce-scatter.3.cloned.1.call-update) | async-done | bytes 6291472 | tf_op jit(solution)/shard_map/reduce_scatter | solution.py:26
  61.6 0.0 reduce-scatter.5.cloned.1.call-update
  61.6 0.0 all-gather.7.cloned.1.call-start
  61.8 0.6 multiply_convert_fusion.2
  62.4 0.0 all-gather.7.cloned.1.call-update
  62.4 114.4 %reduce-scatter.5.cloned.1.call-done = f32[1,32,3072]{2,1,0:T(8,128)} async-done(((f32[16,32,3072]{2,1,0:T(8,128)}), f32[1,32,3072]{2,1,0:T(8,128)}) %reduce-scatter.5.cloned.1.call-update) | async-done | bytes 393232 | tf_op jit(solution)/shard_map/reduce_scatter | solution.py:27
  176.9 1.0 multiply_bitcast_fusion
  177.9 13.7 %all-gather = f32[12288]{0:T(1024)S(1)} all-gather(f32[3072]{0:T(1024)S(1)} %get-tuple-element.6), channel_id=2, replica_groups=mesh['batch_0'=4,'batch_1'=4,'batch_2'=2,'gene_0'=4,'gene_1'=2] {'batch_0'}, dimensions={0}, use_global_device_ids=true | all-gather | bytes 61440 | tf_op jit(solution)/shard_map/all_gather | solution.py:32
  191.7 13.1 %all-gather.1 = f32[12288]{0:T(1024)S(1)} all-gather(f32[3072]{0:T(1024)S(1)} %reduce_sum.91), channel_id=3, replica_groups=mesh['batch_0'=4,'batch_1'=4,'batch_2'=2,'gene_0'=4,'gene_1'=2] {'batch_1'}, dimensions={0}, use_global_device_ids=true | all-gather | bytes 61440 | tf_op jit(solution)/shard_map/all_gather | solution.py:32
  204.8 1.8 all-gather.2
  206.7 12.0 %all-gather.3 = f32[12288]{0:T(1024)S(1)} all-gather(f32[3072]{0:T(1024)S(1)} %reduce_sum.93), channel_id=5, replica_groups=mesh['batch_0'=4,'batch_1'=4,'batch_2'=2,'gene_0'=4,'gene_1'=2] {'gene_0'}, dimensions={0}, use_global_device_ids=true | all-gather | bytes 61440 | tf_op jit(solution)/shard_map/all_gather | solution.py:32
  218.7 4.4 %all-gather.4 = f32[6144]{0:T(1024)S(1)} all-gather(f32[3072]{0:T(1024)S(1)} %reduce_sum.94), channel_id=6, replica_groups=mesh['batch_0'=4,'batch_1'=4,'batch_2'=2,'gene_0'=4,'gene_1'=2] {'gene_1'}, dimensions={0}, use_global_device_ids=true | all-gather | bytes 36864 | tf_op jit(solution)/shard_map/all_gather | solution.py:32
  223.2 0.1 copy.12
  223.3 0.2 fusion.4
  223.5 0.3 multiply_reduce_fusion
  223.9 0.3 multiply_convert_fusion.1
  224.2 0.0 all-gather.7.cloned.1.call-done
  224.2 5.7 %multiply_convert_fusion = bf16[768,4096]{1,0:T(8,128)(2,1)} fusion(bf16[768,128]{1,0:T(8,128)(2,1)S(1)} %bitcast.25, bf16[128,4096]{1,0:T(8,128)(2,1)} %all-gather.7.cloned.1.call-done), kind=kOutput, calls=%fused_computation | convolution fusion | flops 811597824 | bytes 7536640 | tf_op jit(solution)/shard_map/dot_general | solution.py:79
  (19 shorter events, 0.4 us)
Async XLA Ops:
  7.4 54.2 %reduce-scatter.3.cloned.1.call-start = ((), (), s32[]{:S(2)}) async-start(), calls=%async_computation.2 | async-start | bytes 18874368 | tf_op jit(solution)/shard_map/reduce_scatter | solution.py:26
  31.5 30.1 %copy-start = (s32[128,128]{1,0:T(8,128)S(1)}, s32[128,128]{1,0:T(8,128)}, u32[]{:S(2)}) copy-start(s32[128,128]{1,0:T(8,128)} %param.9) | copy-start | bytes 196612
  31.6 145.3 %reduce-scatter.5.cloned.1.call-start = ((), (), s32[]{:S(2)}) async-start(), calls=%async_computation.3 | async-start | bytes 6684672 | tf_op jit(solution)/shard_map/reduce_scatter | solution.py:27
  61.6 162.6 %all-gather.7.cloned.1.call-start = ((), (), s32[]{:S(2)}) async-start(), calls=%async_computation.4 | async-start | bytes 1081344 | tf_op jit(solution)/shard_map/all_gather | solution.py:78
Sparse Core Ops, SparseCore 0:
  31.7 29.8 reduce-scatter.2
  65.3 111.5 reduce-scatter.4
Sparse Core Ops, SparseCore 1:
  64.6 63.7 all-gather.6
